TPU v7x, 128 devices: a whole 4x4x4 slice. The times are simulated.
128 devices in a mesh: tau: 8 (over x, core), tile: 16 (over z, y).
Axes of the slice: x: 4, y: 4, z: 4, core: 2. Of those that a mesh axis runs over, the one named last changes fastest.
Arguments:
- occupied: bfloat16 [8, 2048, 128, 128], P('tau', 'tile'), may hold values from -6 to 6
- virtual: bfloat16 [8, 2048, 128, 128], P('tau', 'tile'), may hold values from -0.125 to 0.125
- cos_weights: float32 [4, 8], replicated, may hold values from -1 to 1
- pair_occ: int32 [3072, 16], P('tile'), may hold values from 0 to 127
- pair_virt: int32 [3072, 16], P('tile'), may hold values from 0 to 127
- partial_target_tile: int32 [3072], P('tile'), may hold values from 0 to 511, as said below
Outputs:
- spectrum: float32 [4, 512, 128, 128], P(None, 'tile', 'tau')
Inputs may be any that keep to these rules, and one draw needn't show every extreme that they name: `partial_target_tile`: within each aligned block of 192 entries, no owner (values d * 32 to (d + 1) * 32 - 1 for owner d) is named more than 24 times; one owner is named exactly 24 times in every block.
All inputs are finite; a program needn't handle non-finite values.
Results may differ from a plain program's by a relative error of at most 0.0003.
Values sent between devices are 32-bit elements; how exact they have to be, the bound alone decides.
A program may use at most 192 MiB of HBM per device.

v0:
```python
import math

import jax
import jax.numpy as jnp
from jax import lax
from jax.sharding import PartitionSpec as P

CHI_DEV = 32


def in_one_piece(arrays, axis, split_dim, concat_dim, along):
    columns = [a.reshape(*a.shape[:along], -1) for a in arrays]
    both = jnp.concatenate(columns, axis=along)
    out, at, gathered = (
        lax.all_to_all(both, axis, split_axis=split_dim, concat_axis=concat_dim, tiled=True),
        0,
        [],
    )
    for a, column in zip(arrays, columns):
        piece = out[..., at : at + column.shape[along]]
        gathered.append(piece.reshape(*piece.shape[:along], *a.shape[along:]))
        at += column.shape[along]
    return tuple(gathered)


def block_products(occupied, virtual, occ_index, virt_index, groups):
    tau_count = occupied.shape[0]
    tile_size = occupied.shape[2]
    rows = tile_size // groups
    part_count = occ_index.shape[0]
    terms = occ_index.shape[1]
    group = math.gcd(part_count, 8)
    count = part_count // group
    empty = jnp.zeros((groups, part_count, tau_count, rows, tile_size), jnp.float32)

    def one_block(block, result):
        first = block * group
        occ_rows = lax.dynamic_slice_in_dim(occ_index, first, group, 0)
        virt_rows = lax.dynamic_slice_in_dim(virt_index, first, group, 0)
        left = jnp.take(occupied[0], occ_rows, axis=0)
        right = jnp.take(virtual[0], virt_rows, axis=0)
        left = left.reshape(group, terms, groups, rows, tile_size)
        pieces = [jnp.einsum("bjgrk,bjkc->gbrc", left, right, preferred_element_type=jnp.float32)]
        stacked = jnp.stack(pieces, axis=2)
        return lax.dynamic_update_slice_in_dim(result, stacked, first, 1)

    return lax.fori_loop(0, count, one_block, empty)


def slot_layout(partial_target_tile, chi_dev, owners, capacity):
    owner = partial_target_tile // chi_dev
    member = (owner[:, None] == jnp.arange(owners, dtype=jnp.int32)[None, :]).astype(jnp.int32)
    before = jnp.cumsum(member, axis=0) - member
    rank = jnp.sum(before * member, axis=1)
    position = owner * capacity + rank
    places = jnp.arange(owners * capacity, dtype=jnp.int32)
    match = position[:, None] == places[None, :]
    filled = jnp.any(match, axis=0)
    source = jnp.sum(
        jnp.where(match, jnp.arange(partial_target_tile.shape[0], dtype=jnp.int32)[:, None], 0),
        axis=0,
    )
    local = jnp.sum(jnp.where(match, (partial_target_tile % chi_dev)[:, None], 0), axis=0)
    slot_ids = jnp.where(filled, local, -1).astype(jnp.float32)
    return (source, filled, slot_ids)


def body(occupied, virtual, cos_weights, pair_occ, pair_virt, partial_target_tile):
    owners = lax.axis_size("tile")
    groups = lax.axis_size("tau")
    part_count = pair_occ.shape[0]
    capacity = 2 * part_count // owners
    chi_dev = CHI_DEV
    tau_count = occupied.shape[0]
    tile_size = occupied.shape[2]
    source, filled, slot_ids = slot_layout(partial_target_tile, chi_dev, owners, capacity)
    mask = filled.astype(jnp.float32)
    rows = tile_size // groups
    partial_value = block_products(occupied, virtual, pair_occ, pair_virt, groups)
    slots = source.shape[0]
    outgoing = jnp.take(partial_value, source, axis=1) * mask[None, :, None, None, None]
    split_rows = outgoing.reshape(groups * slots, tau_count, rows, tile_size)
    repeated_ids = jnp.tile(slot_ids, groups)
    incoming, arrived = in_one_piece((split_rows, repeated_ids), ("tau", "tile"), 0, 0, 1)
    incoming = incoming.reshape(groups, slots, tau_count * rows * tile_size)
    arrived = arrived.reshape(groups, slots)
    selector = (
        arrived[:, None, :] == jnp.arange(chi_dev, dtype=jnp.float32)[None, :, None]
    ).astype(jnp.float32)
    chi_time = jnp.einsum("xcs,xsf->cxf", selector, incoming, precision=lax.Precision.HIGHEST)
    chi_time = chi_time.reshape(chi_dev, groups * tau_count, rows, tile_size)
    return jnp.einsum("kt,ctrd->kcrd", cos_weights, chi_time, precision=lax.Precision.HIGHEST)


def solution(mesh):
    in_specs = (
        P("tau", "tile", None, None),
        P("tau", "tile", None, None),
        P(),
        P("tile", None),
        P("tile", None),
        P("tile"),
    )
    out_specs = P(None, "tile", "tau", None)
    return jax.shard_map(body, mesh=mesh, in_specs=in_specs, out_specs=out_specs, check_vma=False)
```

profile of v0, /device:TPU:1, one launch (start us, length us, event | category | flops | bytes accessed | tf_op | source)
XLA Modules:
  0.0 955.5 jit_solution(7878079829436881421)
XLA Ops:
  4.7 6.2 broadcast_in_dim.61
  10.8 504.4 %while.13 = (s32[]{:T(128)}, f32[8,192,1,16,128]{4,3,0,1,2:T(8,128)}, bf16[1,128,128,128]{3,2,1,0:T(8,128)(2,1)}, s32[192,16]{1,0:T(8,128)S(1)}, bf16[1,128,128,...) while((s32[]{:T(128)}, ...), condition=%wide.region_5.7_spmd, body=%wide.region_4.6_spmd.sunk | while | flops 541068800 | bytes 34093720 | solution.py:47
  11.0 5.2 gather_fusion
  20.8 5.2 gather_fusion.1
  26.1 5.8 fusion.31
  32.1 5.2 gather_fusion
  41.9 5.2 gather_fusion.1
  47.1 5.8 fusion.31
  53.2 5.2 gather_fusion
  68.2 5.8 fusion.31
  74.2 5.2 gather_fusion
  89.2 5.8 fusion.31
  95.2 5.2 gather_fusion
  105.0 5.2 gather_fusion.1
  110.2 5.8 fusion.31
  116.2 5.2 gather_fusion
  131.2 5.8 fusion.31
  137.2 5.2 gather_fusion
  152.3 5.8 fusion.31
  158.2 5.2 gather_fusion
  168.0 5.2 gather_fusion.1
  173.2 5.8 fusion.31
  179.2 5.2 gather_fusion
  189.0 5.2 gather_fusion.1
  194.3 5.8 fusion.31
  200.2 5.2 gather_fusion
  215.3 5.8 fusion.31
  221.3 5.2 gather_fusion
  236.3 5.8 fusion.31
  242.3 5.2 gather_fusion
  257.3 5.8 fusion.31
  263.3 5.2 gather_fusion
  278.3 5.8 fusion.31
  284.3 5.2 gather_fusion
  299.4 5.8 fusion.31
  305.3 5.2 gather_fusion
  315.1 5.2 gather_fusion.1
  320.4 5.8 fusion.31
  326.3 5.2 gather_fusion
  341.4 5.8 fusion.31
  347.3 5.2 gather_fusion
  362.4 5.8 fusion.31
  368.3 5.2 gather_fusion
  383.4 5.8 fusion.31
  389.4 5.2 gather_fusion
  404.4 5.8 fusion.31
  410.4 5.2 gather_fusion
  425.4 5.8 fusion.31
  431.4 5.2 gather_fusion
  446.4 5.8 fusion.31
  452.4 5.2 gather_fusion
  467.4 5.8 fusion.31
  473.4 5.2 gather_fusion
  488.4 5.8 fusion.31
  494.4 5.2 gather_fusion
  509.4 5.8 fusion.31
  515.2 19.4 %gather_fusion.2 = f32[384,8,16,128]{3,2,1,0:T(8,128)} fusion(f32[8,192,16,128]{3,2,0,1:T(8,128)} %bitcast.82, s32[1024]{0:T(1024)S(1)} %pad_clamp_fusion.2), kind=kCustom, calls=%fused_computation.2 | custom fusion | bytes 50333184 | tf_op jit(solution)/shard_map/jit(_take)/gather | solution.py:81
  534.6 17.2 %copy.37 = f32[8,384,16,128]{3,2,1,0:T(8,128)} copy(f32[8,384,16,128]{3,2,0,1:T(8,128)} %bitcast.90) | data formatting | bytes 50331648 | tf_op jit(solution)/shard_map/jit(_take)/gather | solution.py:81
  551.8 26.8 %gather.10 = f32[128,24,2048]{2,1,0:T(8,128)} reshape(f32[8,384,16,128]{3,2,1,0:T(8,128)} %copy.37) | data formatting | bytes 50331648 | tf_op jit(solution)/shard_map/jit(_take)/gather | solution.py:81
  578.6 17.3 %select_multiply_fusion = f32[128,24,2048]{2,1,0:T(8,128)} fusion(f32[128,24,2048]{2,1,0:T(8,128)} %gather.10, f32[128,24]{1,0:T(8,128)S(1)} %bitcast.93, pred[128,24]{1,0:T(8,128)(4,1)S(1)} %bitcast.94), kind=kLoop, calls=%fused_computation.19 | loop fusion | flops 12582912 | bytes 50347008 | tf_op jit(solution)/shard_map/mul | solution.py:81
  595.9 9.4 pad_maximum_fusion
  605.3 312.5 %all_to_all.9 = f32[128,24,2049]{2,1,0:T(8,128)} all-to-all(f32[128,24,2049]{2,1,0:T(8,128)S(1)} %pad_maximum_fusion), channel_id=1, replica_groups=mesh['tau'=8,'tile'=16] {'tau','tile'}, dimensions={0} | all-to-all | bytes 50356224 | tf_op jit(solution)/shard_map/all_to_all | solution.py:15
  919.7 17.4 %slice.28 = f32[3072,2048]{1,0:T(8,128)} slice(f32[3072,2049]{1,0:T(8,128)} %bitcast.84), slice={[0:3072], [0:2048]} | slice | bytes 50331648 | tf_op jit(solution)/shard_map/slice | solution.py:20
  937.1 13.9 %fusion.17 = f32[8,2048,32]{1,2,0:T(8,128)S(1)} fusion(f32[8,384,2048]{2,1,0:T(8,128)} %bitcast.89, f32[8,384]{1,0:T(8,128)S(1)} %eq.59), kind=kOutput, calls=%fused_computation.25 | convolution fusion | flops 2416017408 | bytes 27275264 | tf_op jit(solution)/shard_map/xcs,xsf->cxf/dot_general | solution.py:90
  (197 shorter events, 219.0 us)
Async XLA Ops:
  0.0 951.4 %copy-start = (f32[4,8]{1,0:T(4,128)S(1)}, f32[4,8]{1,0:T(4,128)}, u32[]{:S(2)}) copy-start(f32[4,8]{1,0:T(4,128)} %param.12) | copy-start | bytes 388
where the time goes:
time: 962 us; the launch traced here: 956 us
  local copies, waits for them, and re-layouts  349 us (36%)
  blocking collectives  313 us (33%)
  matrix products  156 us (16%)
  other arithmetic  138 us (14%)
    all_to_all x1, blocking collectives, in_one_piece(): lax.all_to_all(both, axis, split_axis=split_dim, concat_axis=concat_dim,...  313 us
    dot_general x24, matrix products, one_block(): jnp.einsum('bjgrk,bjkc->gbrc', left, right, preferred_element_type=jnp.fl...  139 us
    gather x24, local copies, waits for them, and re-layouts, one_block(): left = jnp.take(occupied[0], occ_rows, axis=0)  126 us
    gather x24, local copies, waits for them, and re-layouts, one_block(): right = jnp.take(virtual[0], virt_rows, axis=0)  126 us
    select_n x24, other arithmetic, one_block(): left = jnp.take(occupied[0], occ_rows, axis=0)  109 us
    gather x3, local copies, waits for them, and re-layouts, body(): jnp.take(partial_value, source, axis=1) * mask[None, :, None, None, None]  63.4 us
    slice x2, local copies, waits for them, and re-layouts, in_one_piece(): piece = out[..., at:at + column.shape[along]]  19.3 us

commit v1 on v0

v1 whole, which is shorter than its diff:
```python
import functools

import jax
import jax.numpy as jnp
from jax import lax
from jax.experimental import pallas as pl
from jax.experimental.pallas import tpu as pltpu
from jax.sharding import PartitionSpec as P

CHI_DEV = 32
MESH = pl.DeviceIdType.MESH


def chunks_of(cap):
    return 8 if cap % 8 == 0 else 2


def tables(target, chi_dev, owners, cap, chunks):
    parts = target.shape[0]
    deep = cap // chunks
    index = jnp.arange(parts, dtype=jnp.int32)
    owner = target // chi_dev
    key = owner * parts + index
    position = jnp.sum((key[None, :] < key[:, None]).astype(jnp.int32), axis=1)
    hit = position[:, None] == index[None, :]
    order = jnp.sum(jnp.where(hit, index[:, None], 0), axis=0)
    names = jnp.arange(owners, dtype=jnp.int32)
    first = jnp.sum((owner[:, None] < names[None, :]).astype(jnp.int32), axis=0)
    last = jnp.sum((owner[:, None] <= names[None, :]).astype(jnp.int32), axis=0)
    q = jnp.arange(chunks, dtype=jnp.int32)[:, None, None]
    k = jnp.arange(deep, dtype=jnp.int32)[None, None, :]
    place = first[None, :, None] + (q - first[None, :, None]) % chunks + chunks * k
    filled = place < last[None, :, None]
    source = jnp.minimum(place // chunks, parts // chunks - 1)
    flat = place.reshape(-1)
    local = jnp.sum(jnp.where(position[:, None] == flat[None, :], (target % chi_dev)[:, None], 0), axis=0)
    slot_ids = jnp.where(filled.reshape(-1), local, -1).astype(jnp.float32)
    slot_ids = slot_ids.reshape(chunks, owners, deep).transpose(1, 0, 2).reshape(owners, 1, cap)
    slot_ids = jnp.broadcast_to(jnp.pad(slot_ids, ((0, 0), (0, 0), (0, 128 - cap))), (owners, 8, 128))
    return order, source.reshape(-1), slot_ids


def kernel(
    cfg, order, pair_occ, pair_virt, source, weights, occ, virt, ids, out,
    stage, xrecv, spec, ysend, yrecv, idrecv, idwide,
    xs, xr, ys, yr, ids_s, ids_r,
):
    T, B, Q, NB, LX, LY, terms = cfg
    n = stage.shape[2]
    rows, cols = stage.shape[3:]
    freqs, chi = out.shape[:2]
    deep = yrecv.shape[2]
    blocks = yrecv.shape[3]
    t = lax.axis_index("tau")
    b = lax.axis_index("tile")

    barrier = pltpu.get_barrier_semaphore()
    for d in range(1, T):
        pl.semaphore_signal(barrier, inc=1, device_id=(lax.rem(t + d, T), b), device_id_type=MESH)
    for d in range(1, B):
        pl.semaphore_signal(barrier, inc=1, device_id=(t, lax.rem(b + d, B)), device_id_type=MESH)

    def compute(s):
        buf = lax.rem(s, NB)

        def one(i, carry):
            p = order[s + Q * i] * terms
            left = jnp.concatenate([occ[pair_occ[p + j]] for j in range(terms)], axis=1)
            right = jnp.concatenate([virt[pair_virt[p + j]] for j in range(terms)], axis=0)
            product = jnp.dot(left, right, preferred_element_type=jnp.float32)
            for g in range(T):
                stage[buf, g, i] = product[g * rows : (g + 1) * rows]
            return carry

        lax.fori_loop(0, n, one, 0)

    def x_copy(s, d):
        buf = lax.rem(s, NB)
        to = lax.rem(t + d, T)
        return pltpu.make_async_remote_copy(
            src_ref=stage.at[buf, to],
            dst_ref=xrecv.at[s, d - 1],
            send_sem=xs.at[buf],
            recv_sem=xr.at[s],
            device_id=(to, b),
            device_id_type=MESH,
        )

    def x_all(s):
        return pltpu.make_async_remote_copy(
            src_ref=stage.at[lax.rem(s, NB), pl.ds(0, T - 1)],
            dst_ref=xrecv.at[s],
            send_sem=xs.at[lax.rem(s, NB)],
            recv_sem=xr.at[s],
            device_id=(lax.rem(t + 1, T), b),
            device_id_type=MESH,
        )

    def y_copy(q, d):
        buf = lax.rem(q, NB)
        return pltpu.make_async_remote_copy(
            src_ref=ysend.at[buf, d - 1],
            dst_ref=yrecv.at[q, d],
            send_sem=ys.at[buf],
            recv_sem=yr.at[q],
            device_id=(t, lax.rem(b + d, B)),
            device_id_type=MESH,
        )

    def y_all(q):
        return pltpu.make_async_remote_copy(
            src_ref=ysend.at[lax.rem(q, NB)],
            dst_ref=yrecv.at[q, pl.ds(1, B - 1)],
            send_sem=ys.at[lax.rem(q, NB)],
            recv_sem=yr.at[q],
            device_id=(t, lax.rem(b + 1, B)),
            device_id_type=MESH,
        )

    def id_copy(d):
        to = lax.rem(b + d, B)
        return pltpu.make_async_remote_copy(
            src_ref=ids.at[to],
            dst_ref=idrecv.at[d],
            send_sem=ids_s.at[d],
            recv_sem=ids_r.at[d],
            device_id=(t, to),
            device_id_type=MESH,
        )

    def transform(q):
        buf = lax.rem(q, NB)
        w = [[weights[k * T + lax.rem(t + T - d, T)] for k in range(freqs)] for d in range(T)]

        def one(i, carry):
            total = [None] * freqs
            for d in range(T):
                v = stage[buf, t, i] if d == 0 else xrecv[q, d - 1, i]
                for k in range(freqs):
                    term = v * w[d][k]
                    total[k] = term if total[k] is None else total[k] + term
            for k in range(freqs):
                for r in range(rows // 8):
                    spec[i, k * (rows // 8) + r] = total[k][r * 8 : r * 8 + 8]
            return carry

        lax.fori_loop(0, n, one, 0)

    def pack(q):
        buf = lax.rem(q, NB)
        for k in range(deep):
            yrecv[q, 0, k] = spec[source[(q * B + b) * deep + k]]

        def one(d, carry):
            at = (q * B + lax.rem(b + d, B)) * deep
            for k in range(deep):
                ysend[buf, d - 1, k] = spec[source[at + k]]
            return carry

        lax.fori_loop(1, B, one, 0)

    def widen():
        def one(d, carry):
            v = idrecv[d]
            for s in range(Q * deep):
                idwide[s // deep, d, s % deep] = jnp.broadcast_to(v[:, s : s + 1], v.shape)
            return carry

        lax.fori_loop(0, B, one, 0)

    def reduce(q):
        def one(c, carry):
            want = c.astype(jnp.float32)
            total = None
            for d in range(B):
                for k in range(deep):
                    same = idwide[q, d, k] == want
                    part = jnp.where(same[None], yrecv[q, d, k], 0.0)
                    total = part if total is None else total + part
            total = total.reshape(freqs, rows, cols)
            out[:, c] = jnp.where(q > 0, out[:, c], 0.0) + total
            return carry

        lax.fori_loop(0, chi, one, 0)

    def step(s, carry):
        @pl.when(s < Q)
        def _():
            @pl.when(s >= NB)
            def _():
                x_all(s - NB).wait_send()

            compute(s)

            @pl.when(s == 0)
            def _():
                pl.semaphore_wait(barrier, T - 1 + B - 1)
                for d in range(1, B):
                    id_copy(d).start()

            for d in range(1, T):
                x_copy(s, d).start()

        @pl.when(s == LX)
        def _():
            idrecv[0] = ids[b]
            for d in range(1, B):
                id_copy(d).wait()
            widen()

        @pl.when(jnp.logical_and(s >= LX, s < Q + LX))
        def _():
            q = s - LX
            x_all(q).wait_recv()
            transform(q)

            @pl.when(q >= NB)
            def _():
                y_all(q - NB).wait_send()

            pack(q)
            for d in range(1, B):
                y_copy(q, d).start()

        @pl.when(s >= LX + LY)
        def _():
            q = s - LX - LY
            y_all(q).wait_recv()
            reduce(q)

        return carry

    lax.fori_loop(0, Q + LX + LY, step, 0)
    for i in range(min(NB, Q)):
        x_all(Q - 1 - i).wait_send()
        y_all(Q - 1 - i).wait_send()


def body(occupied, virtual, cos_weights, pair_occ, pair_virt, partial_target_tile):
    B = lax.axis_size("tile")
    T = lax.axis_size("tau")
    parts, terms = pair_occ.shape
    cap = 2 * parts // B
    freqs = cos_weights.shape[0]
    slots, size = occupied.shape[1:3]
    rows = size // T
    Q = chunks_of(cap)
    NB, LX, LY = min(4, Q), 2, 2
    n, deep, blocks = parts // Q, cap // Q, freqs * rows // 8
    order, source, ids = tables(partial_target_tile, CHI_DEV, B, cap, Q)
    f32 = jnp.float32
    smem = pl.BlockSpec(memory_space=pltpu.SMEM)
    vmem = pl.BlockSpec(memory_space=pltpu.VMEM)
    dma = pltpu.SemaphoreType.DMA
    return pl.pallas_call(
        functools.partial(kernel, (T, B, Q, NB, LX, LY, terms)),
        out_shape=jax.ShapeDtypeStruct((freqs, CHI_DEV, rows, size), f32),
        in_specs=[smem] * 5 + [vmem] * 3,
        out_specs=vmem,
        scratch_shapes=[
            pltpu.VMEM((NB, T, n, rows, size), f32),
            pltpu.VMEM((Q, T - 1, n, rows, size), f32),
            pltpu.VMEM((n, blocks, 8, size), f32),
            pltpu.VMEM((NB, B - 1, deep, blocks, 8, size), f32),
            pltpu.VMEM((Q, B, deep, blocks, 8, size), f32),
            pltpu.VMEM((B, 8, 128), f32),
            pltpu.VMEM((Q, B, deep, 8, 128), f32),
            dma((NB,)),
            dma((Q,)),
            dma((NB,)),
            dma((Q,)),
            dma((B,)),
            dma((B,)),
        ],
        compiler_params=pltpu.CompilerParams(
            collective_id=0, has_side_effects=True, vmem_limit_bytes=62 * 1024 * 1024
        ),
        name="products",
    )(
        order,
        pair_occ.reshape(-1),
        pair_virt.reshape(-1),
        source,
        cos_weights.reshape(-1),
        occupied.reshape(slots, size, size),
        virtual.reshape(slots, size, size),
        ids,
    )


def solution(mesh):
    in_specs = (
        P("tau", "tile", None, None),
        P("tau", "tile", None, None),
        P(),
        P("tile", None),
        P("tile", None),
        P("tile"),
    )
    out_specs = P(None, "tile", "tau", None)
    return jax.shard_map(body, mesh=mesh, in_specs=in_specs, out_specs=out_specs, check_vma=False)
```

time: 962 us -> 198 us (0.21)
  local copies, waits for them, and re-layouts: 349 us -> 7.79 us
  blocking collectives: 313 us -> 0 us
  Pallas kernels: 0 us -> 187 us
  matrix products: 156 us -> 0 us
  other arithmetic: 138 us -> 2.59 us
    gather x51 -> x0, local copies, waits for them, and re-layouts: 315 us -> none  [the longest x24 126 us: one_block(): left = jnp.take(occupied[0], occ_rows, axis=0)]
    all_to_all x1 -> x0, blocking collectives: 313 us -> none  [in_one_piece(): lax.all_to_all(both, axis, split_axis=split_dim, concat_axis=concat_dim,...]
    pallas_call x0 -> x1, Pallas kernels: none -> 187 us  [body(): pl.pallas_call(functools.partial(kernel, (T, B, Q, NB, LX, LY, terms)), o...]
    dot_general x26 -> x0, matrix products: 156 us -> none  [the longest x24 139 us: one_block(): jnp.einsum('bjgrk,bjkc->gbrc', left, right, preferred_element_type=jnp.fl...]
    select_n x26 -> x0, other arithmetic: 110 us -> none  [the longest x24 109 us: one_block(): left = jnp.take(occupied[0], occ_rows, axis=0)]
    slice x3 -> x0, local copies, waits for them, and re-layouts: 19.5 us -> none  [the longest x2 19.3 us: in_one_piece(): piece = out[..., at:at + column.shape[along]]]
    mul x1, other arithmetic: 17.3 us -> 0.01 us  [tables(): chunks * k]
where the time goes in v1:
time: 198 us; the launch traced here: 197 us
  Pallas kernels  187 us (94%)
  local copies, waits for them, and re-layouts  7.79 us (4%)
  other arithmetic  2.59 us (1%)
    pallas_call x1, Pallas kernels, body(): pl.pallas_call(functools.partial(kernel, (T, B, Q, NB, LX, LY, terms)), o...  187 us

profile of v1, /device:TPU:1, one launch (start us, length us, event | category | flops | bytes accessed | tf_op | source)
XLA Modules:
  0.0 197.4 jit_solution(2592010176819438759)
XLA Ops:
  0.0 1.2 reshape.104.weights
  1.3 0.7 iota_add_fusion
  1.9 0.2 convert_reduce_fusion
  2.1 0.7 select_reduce_fusion.1.order
  2.8 0.1 convert_reduce_fusion.1
  3.0 0.1 broadcast_add_fusion
  3.0 0.2 add.68
  3.3 0.1 select_reduce_fusion
  3.4 0.6 fusion.6.source
  4.0 0.2 reduce_sum.52
  4.2 0.1 convert_bitcast_fusion
  4.3 0.1 copy.13
  4.4 0.1 copy.14
  4.5 0.7 broadcast_in_dim.57.ids
  5.1 0.8 copy.11
  5.9 0.7 reshape.102.pair_occ
  6.6 0.8 copy.12
  7.4 0.7 reshape.103.pair_virt
  8.1 187.0 %products.1 = f32[4,32,16,128]{3,2,1,0:T(8,128)} custom-call(s32[192]{0:T(256)} %select_reduce_fusion.1.order, s32[3072]{0:T(1024)} %reshape.102.pair_occ, s32[3072]{0:T(1024)} %reshape.103.pair_virt, s32[384]{0:T(512)} %fusion.6.source, f32[32]{0:T(128)} %reshape.104.weights, bf16[128,128,128]{2,1,0:T(8,128)(2,1)} %bitcast.8, ...), custom_call_target="tpu_custom_call" | custom-call | tf_op jit(solution)/shard_map/products/pallas_call | solution.py:255
  195.1 2.3 %copy.16 = f32[4,32,16,128]{3,2,1,0:T(8,128)} copy(f32[4,32,16,128]{3,2,1,0:T(8,128)} %products.1) | data formatting | bytes 2097152
  (4 shorter events, 0.0 us)

commit v2 on v1

v2 whole, which is shorter than its diff:
```python
import functools
import math

import jax
import jax.numpy as jnp
from jax import lax
from jax.experimental import pallas as pl
from jax.experimental.pallas import tpu as pltpu
from jax.sharding import PartitionSpec as P

CHI_DEV = 32
MESH = pl.DeviceIdType.MESH


def chunks_of(cap):
    return 24 if cap % 24 == 0 else cap


def tables(target_ref, padded, table, idrow, Q, owners, chi_dev):
    i32 = jnp.int32
    N, M = target_ref.shape[1], padded.shape[1]
    S = Q * owners
    padded[...] = jnp.full(padded.shape, owners * chi_dev, i32)
    padded[:, pl.ds(0, N)] = target_ref[...]
    target = padded[...]
    up = lax.broadcasted_iota(i32, (M, M), 0)
    across = lax.broadcasted_iota(i32, (M, M), 1)

    def column(row):
        return jnp.transpose(jnp.broadcast_to(row, (8, M)))[:, 0:1]

    def total(chosen, value):
        return jnp.sum(jnp.where(chosen, value, 0), axis=0, keepdims=True)

    key = (target // chi_dev) * M + lax.broadcasted_iota(i32, (1, M), 1)
    target_col = column(target)
    own_col, local_col = target_col // chi_dev, target_col % chi_dev
    key_col = own_col * M + lax.broadcasted_iota(i32, (M, 1), 0)
    place_col = column(total(key_col < key, jnp.ones((M, M), i32)))
    order = total(place_col == across, up)
    slot = lax.broadcasted_iota(i32, (1, S), 1)
    name = slot % owners
    chunk = slot // owners
    one = jnp.ones((M, S), i32)
    first = total(own_col < name, one)
    last = total(own_col <= name, one)
    offset = chunk - first % Q
    place = first + jnp.where(offset < 0, offset + Q, offset)
    found = total(place_col == place, jnp.broadcast_to(local_col, (M, S)))
    idrow[...] = jnp.where(place < last, found, -1).astype(jnp.float32)
    table[pl.ds(0, 1), pl.ds(0, M)] = jnp.minimum(order, N - 1)
    table[pl.ds(1, 1), pl.ds(0, S)] = jnp.minimum(place // Q, N // Q - 1)


def around(me, offset, sizes):
    (a, b), (big, small) = offset, sizes
    return lax.rem(me // small + a, big) * small + lax.rem(me + b, small)


def offsets(sizes):
    every = [(a, b) for a in range(sizes[0]) for b in range(sizes[1])]
    far = lambda v, n: min(v, n - v)
    return sorted(every, key=lambda o: (far(o[0], sizes[0]) + far(o[1], sizes[1]), o[0] * o[1] > 0, o[0] + o[1], o))


def back(offset, sizes):
    return tuple((n - v) % n for v, n in zip(offset, sizes))


def kernel(
    cfg, pair_occ, pair_virt, weights, target, occ_hbm, virt_hbm, out,
    occ, virt, stage, xrecv, spec, ysend, yrecv, padded, table, smem, idrow, idrecv, idwide,
    xs, xr, ys, yr, ids_s, ids_r, load,
):
    tau, tile, Q, NB, LX, LY = cfg
    T, B = tau[0] * tau[1], tile[0] * tile[1]
    terms = pair_occ.shape[0]
    n = stage.shape[2]
    rows, cols = stage.shape[3:]
    freqs, chi = out.shape[:2]
    t = lax.axis_index("tau")
    b = lax.axis_index("tile")
    near_t, near_b = offsets(tau), offsets(tile)

    def tau_at(d):
        return around(t, near_t[d], tau)

    def tile_at(d):
        return around(b, near_b[d], tile)

    loads = [
        pltpu.make_async_copy(occ_hbm, occ, load.at[0]),
        pltpu.make_async_copy(virt_hbm, virt, load.at[1]),
    ]
    for copy in loads:
        copy.start()
    barrier = pltpu.get_barrier_semaphore()
    for d in range(1, T):
        pl.semaphore_signal(barrier, inc=1, device_id=(tau_at(d), b), device_id_type=MESH)
    for d in range(1, B):
        pl.semaphore_signal(barrier, inc=1, device_id=(t, tile_at(d)), device_id_type=MESH)
    tables(target, padded, table, idrow, Q, B, chi)
    down = pltpu.make_async_copy(table, smem, load.at[2])
    down.start()
    down.wait()
    for copy in loads:
        copy.wait()

    def compute(s):
        buf = lax.rem(s, NB)

        def one(i, carry):
            p = smem[0, s + Q * i]
            left = jnp.concatenate([occ[pair_occ[j, p]] for j in range(terms)], axis=1)
            right = jnp.concatenate([virt[pair_virt[j, p]] for j in range(terms)], axis=0)
            product = jnp.dot(left, right, preferred_element_type=jnp.float32)
            for g in range(T):
                stage[buf, g, i] = product[g * rows : (g + 1) * rows]
            return carry

        lax.fori_loop(0, n, one, 0)

    def x_copy(s, d):
        buf = lax.rem(s, NB)
        to = tau_at(d)
        return pltpu.make_async_remote_copy(
            src_ref=stage.at[buf, to],
            dst_ref=xrecv.at[s, d - 1],
            send_sem=xs.at[buf],
            recv_sem=xr.at[s],
            device_id=(to, b),
            device_id_type=MESH,
        )

    def x_all(s):
        return pltpu.make_async_remote_copy(
            src_ref=stage.at[lax.rem(s, NB), pl.ds(0, T - 1)],
            dst_ref=xrecv.at[s],
            send_sem=xs.at[lax.rem(s, NB)],
            recv_sem=xr.at[s],
            device_id=(tau_at(1), b),
            device_id_type=MESH,
        )

    def y_copy(q, d):
        buf = lax.rem(q, NB)
        return pltpu.make_async_remote_copy(
            src_ref=ysend.at[buf, d - 1],
            dst_ref=yrecv.at[q, d],
            send_sem=ys.at[buf],
            recv_sem=yr.at[q],
            device_id=(t, tile_at(d)),
            device_id_type=MESH,
        )

    def y_all(q):
        return pltpu.make_async_remote_copy(
            src_ref=ysend.at[lax.rem(q, NB)],
            dst_ref=yrecv.at[q, pl.ds(1, B - 1)],
            send_sem=ys.at[lax.rem(q, NB)],
            recv_sem=yr.at[q],
            device_id=(t, tile_at(1)),
            device_id_type=MESH,
        )

    def id_copy(d):
        return pltpu.make_async_remote_copy(
            src_ref=idrow,
            dst_ref=idrecv.at[d],
            send_sem=ids_s.at[d],
            recv_sem=ids_r.at[d],
            device_id=(t, tile_at(d)),
            device_id_type=MESH,
        )

    def transform(q):
        buf = lax.rem(q, NB)
        w = [[weights[k, around(t, back(near_t[d], tau), tau)] for k in range(freqs)] for d in range(T)]

        def one(i, carry):
            total = [None] * freqs
            for d in range(T):
                v = stage[buf, t, i] if d == 0 else xrecv[q, d - 1, i]
                for k in range(freqs):
                    term = v * w[d][k]
                    total[k] = term if total[k] is None else total[k] + term
            for k in range(freqs):
                for r in range(rows // 8):
                    spec[i, k * (rows // 8) + r] = total[k][r * 8 : r * 8 + 8]
            return carry

        lax.fori_loop(0, n, one, 0)

    def pack(q):
        buf = lax.rem(q, NB)
        yrecv[q, 0] = spec[smem[1, q * B + b]]
        for d in range(1, B):
            ysend[buf, d - 1] = spec[smem[1, q * B + tile_at(d)]]
            y_copy(q, d).start()

    def widen():
        S = Q * B
        ids = jnp.concatenate([idrecv[d] for d in range(B)], axis=0).astype(jnp.bfloat16)
        slot = lax.broadcasted_iota(jnp.int32, (S, cols), 0)

        def one(q, carry):
            pick = jnp.where(slot == q * B + b, 1.0, 0.0).astype(jnp.bfloat16)
            idwide[q] = jnp.dot(ids, pick, preferred_element_type=jnp.float32)
            return carry

        lax.fori_loop(0, Q, one, 0)

    def reduce(q):
        def one(c, carry):
            want = c.astype(jnp.float32)
            total = None
            for d in range(B):
                same = jnp.broadcast_to(idwide[q, pl.ds(d, 1)], (8, cols)) == want
                part = jnp.where(same[None], yrecv[q, d], 0.0)
                total = part if total is None else total + part
            total = total.reshape(freqs, rows, cols)
            out[:, c] = jnp.where(q > 0, out[:, c], 0.0) + total
            return carry

        lax.fori_loop(0, chi, one, 0)

    def step(s, carry):
        @pl.when(s < Q)
        def _():
            @pl.when(s >= NB)
            def _():
                x_all(s - NB).wait_send()

            compute(s)

            @pl.when(s == 0)
            def _():
                pl.semaphore_wait(barrier, T - 1 + B - 1)
                for d in range(1, B):
                    id_copy(d).start()

            for d in range(1, T):
                x_copy(s, d).start()

        @pl.when(s == LX)
        def _():
            idrecv[0] = idrow[...]
            for d in range(1, B):
                id_copy(d).wait()
            widen()

        @pl.when(jnp.logical_and(s >= LX, s < Q + LX))
        def _():
            q = s - LX
            x_all(q).wait_recv()
            transform(q)

            @pl.when(q >= NB)
            def _():
                y_all(q - NB).wait_send()

            pack(q)

        @pl.when(s >= LX + LY)
        def _():
            q = s - LX - LY
            y_all(q).wait_recv()
            reduce(q)

        return carry

    lax.fori_loop(0, Q + LX + LY, step, 0)
    for i in range(min(NB, Q)):
        x_all(Q - 1 - i).wait_send()
        y_all(Q - 1 - i).wait_send()


def pair_of(size, small):
    return (size // small, small)


def body(occupied, virtual, cos_weights, pair_occ, pair_virt, partial_target_tile):
    B = lax.axis_size("tile")
    T = lax.axis_size("tau")
    parts, terms = pair_occ.shape
    freqs = cos_weights.shape[0]
    slots, size = occupied.shape[1:3]
    rows = size // T
    Q = chunks_of(2 * parts // B)
    NB, LX, LY = min(6, Q), 3, 3
    n, blocks = parts // Q, freqs * rows // 8
    f32 = jnp.float32
    smem = pl.BlockSpec(memory_space=pltpu.SMEM)
    vmem = pl.BlockSpec(memory_space=pltpu.VMEM)
    hbm = pl.BlockSpec(memory_space=pl.ANY)
    dma = pltpu.SemaphoreType.DMA
    full = -(-parts // 128) * 128
    wide = max(full, Q * B)
    return pl.pallas_call(
        functools.partial(kernel, (pair_of(T, 2), pair_of(B, math.isqrt(B)), Q, NB, LX, LY)),
        out_shape=jax.ShapeDtypeStruct((freqs, CHI_DEV, rows, size), f32),
        in_specs=[smem] * 3 + [vmem, hbm, hbm],
        out_specs=vmem,
        scratch_shapes=[
            pltpu.VMEM((slots, size, size), occupied.dtype),
            pltpu.VMEM((slots, size, size), virtual.dtype),
            pltpu.VMEM((NB, T, n, rows, size), f32),
            pltpu.VMEM((Q, T - 1, n, rows, size), f32),
            pltpu.VMEM((n, blocks, 8, size), f32),
            pltpu.VMEM((NB, B - 1, blocks, 8, size), f32),
            pltpu.VMEM((Q, B, blocks, 8, size), f32),
            pltpu.VMEM((1, full), jnp.int32),
            pltpu.VMEM((8, wide), jnp.int32),
            pltpu.SMEM((8, wide), jnp.int32),
            pltpu.VMEM((1, Q * B), f32),
            pltpu.VMEM((B, 1, Q * B), f32),
            pltpu.VMEM((Q, B, size), f32),
            dma((NB,)),
            dma((Q,)),
            dma((NB,)),
            dma((Q,)),
            dma((B,)),
            dma((B,)),
            dma((3,)),
        ],
        compiler_params=pltpu.CompilerParams(
            collective_id=0, has_side_effects=True, vmem_limit_bytes=60 * 1024 * 1024
        ),
        name="products",
    )(
        pair_occ.T,
        pair_virt.T,
        cos_weights,
        partial_target_tile.reshape(1, parts),
        occupied.reshape(slots, size, size),
        virtual.reshape(slots, size, size),
    )


def solution(mesh):
    in_specs = (
        P("tau", "tile", None, None),
        P("tau", "tile", None, None),
        P(),
        P("tile", None),
        P("tile", None),
        P("tile"),
    )
    out_specs = P(None, "tile", "tau", None)
    return jax.shard_map(body, mesh=mesh, in_specs=in_specs, out_specs=out_specs, check_vma=False)
```

time: 198 us -> 167 us (0.84)
  Pallas kernels: 187 us -> 164 us
  local copies, waits for them, and re-layouts: 7.79 us -> 2.29 us
  other arithmetic: 2.59 us -> 0 us
    pallas_call x1, Pallas kernels: 187 us -> 164 us  [body(): pl.pallas_call(functools.partial(kernel, (pair_of(T, 2), pair_of(B, math....]
    reshape x4 -> x0, local copies, waits for them, and re-layouts: 2.64 us -> none  [the longest x1 1.25 us: body(): cos_weights.reshape(-1)]
where the time goes in v2:
time: 167 us; the launch traced here: 166 us
  Pallas kernels  164 us (98%)
  local copies, waits for them, and re-layouts  2.29 us (1%)
    pallas_call x1, Pallas kernels, body(): pl.pallas_call(functools.partial(kernel, (pair_of(T, 2), pair_of(B, math....  164 us

profile of v2, /device:TPU:1, one launch (start us, length us, event | category | flops | bytes accessed | tf_op | source)
XLA Modules:
  0.0 166.3 jit_solution(13417794597385595857)
XLA Ops:
  0.0 164.0 %products.1 = f32[4,32,16,128]{3,2,1,0:T(8,128)} custom-call(s32[16,192]{1,0:T(8,128)} %bitcast.7, s32[16,192]{1,0:T(8,128)} %bitcast.8, f32[4,8]{1,0:T(4,128)} %weights.1, s32[1,192]{1,0:T(1,128)} %bitcast.9, bf16[128,128,128]{2,1,0:T(8,128)(2,1)} %bitcast.5, bf16[128,128,128]{2,1,0:T(8,128)(2,1)} %bitcast.6), custom_call_target="tpu_custom_call" | custom-call | tf_op jit(solution)/shard_map/products/pallas_call | solution.py:299
  164.0 2.3 %copy.8 = f32[4,32,16,128]{3,2,1,0:T(8,128)} copy(f32[4,32,16,128]{3,2,1,0:T(8,128)} %products.1) | data formatting | bytes 2097152

commit v3 on v2

--- a/solution.py
+++ b/solution.py
@@ -9,6 +9,7 @@
 from jax.sharding import PartitionSpec as P
 
 CHI_DEV = 32
+UNROLL = 2
 MESH = pl.DeviceIdType.MESH
 
 
@@ -60,7 +61,7 @@
 def offsets(sizes):
     every = [(a, b) for a in range(sizes[0]) for b in range(sizes[1])]
     far = lambda v, n: min(v, n - v)
-    return sorted(every, key=lambda o: (far(o[0], sizes[0]) + far(o[1], sizes[1]), o[0] * o[1] > 0, o[0] + o[1], o))
+    return every[:1] + sorted(every[1:], reverse=True, key=lambda o: (far(o[0], sizes[0]) + far(o[1], sizes[1]), o[0] * o[1] > 0, o[0] + o[1], o))
 
 
 def back(offset, sizes):
@@ -68,8 +69,8 @@
 
 
 def kernel(
-    cfg, pair_occ, pair_virt, weights, target, occ_hbm, virt_hbm, out,
-    occ, virt, stage, xrecv, spec, ysend, yrecv, padded, table, smem, idrow, idrecv, idwide,
+    cfg, pair_occ_hbm, pair_virt_hbm, weights, target_hbm, occ_hbm, virt_hbm, out,
+    pair_occ, pair_virt, target, occ, virt, stage, xrecv, spec, ysend, yrecv, padded, table, smem, idrow, idrecv, idwide,
     xs, xr, ys, yr, ids_s, ids_r, load,
 ):
     tau, tile, Q, NB, LX, LY = cfg
@@ -88,7 +89,11 @@
     def tile_at(d):
         return around(b, near_b[d], tile)
 
+    names = pltpu.make_async_copy(target_hbm, target, load.at[3])
+    names.start()
     loads = [
+        pltpu.make_async_copy(pair_occ_hbm, pair_occ, load.at[4]),
+        pltpu.make_async_copy(pair_virt_hbm, pair_virt, load.at[5]),
         pltpu.make_async_copy(occ_hbm, occ, load.at[0]),
         pltpu.make_async_copy(virt_hbm, virt, load.at[1]),
     ]
@@ -99,6 +104,7 @@
         pl.semaphore_signal(barrier, inc=1, device_id=(tau_at(d), b), device_id_type=MESH)
     for d in range(1, B):
         pl.semaphore_signal(barrier, inc=1, device_id=(t, tile_at(d)), device_id_type=MESH)
+    names.wait()
     tables(target, padded, table, idrow, Q, B, chi)
     down = pltpu.make_async_copy(table, smem, load.at[2])
     down.start()
@@ -106,26 +112,28 @@
     for copy in loads:
         copy.wait()
 
-    def compute(s):
+    def compute(s, lo, hi):
         buf = lax.rem(s, NB)
 
-        def one(i, carry):
-            p = smem[0, s + Q * i]
-            left = jnp.concatenate([occ[pair_occ[j, p]] for j in range(terms)], axis=1)
-            right = jnp.concatenate([virt[pair_virt[j, p]] for j in range(terms)], axis=0)
-            product = jnp.dot(left, right, preferred_element_type=jnp.float32)
-            for g in range(T):
-                stage[buf, g, i] = product[g * rows : (g + 1) * rows]
+        def some(step, carry):
+            for u in range(UNROLL):
+                i = step * UNROLL + u
+                p = smem[0, s + Q * i]
+                left = jnp.concatenate([occ[pair_occ[j, p]] for j in range(terms)], axis=1)
+                right = jnp.concatenate([virt[pair_virt[j, p]] for j in range(terms)], axis=0)
+                product = jnp.dot(left, right, preferred_element_type=jnp.float32)
+                for g in range(T):
+                    stage[buf, g, i] = product[g * rows : (g + 1) * rows]
             return carry
 
-        lax.fori_loop(0, n, one, 0)
-
-    def x_copy(s, d):
+        lax.fori_loop(lo // UNROLL, hi // UNROLL, some, 0)
+
+    def x_copy(s, d, lo, size):
         buf = lax.rem(s, NB)
         to = tau_at(d)
         return pltpu.make_async_remote_copy(
-            src_ref=stage.at[buf, to],
-            dst_ref=xrecv.at[s, d - 1],
+            src_ref=stage.at[buf, to, pl.ds(lo, size)],
+            dst_ref=xrecv.at[s, d - 1, pl.ds(lo, size)],
             send_sem=xs.at[buf],
             recv_sem=xr.at[s],
             device_id=(to, b),
@@ -231,16 +239,23 @@
             def _():
                 x_all(s - NB).wait_send()
 
-            compute(s)
-
             @pl.when(s == 0)
             def _():
+                compute(s, 0, n // 2)
                 pl.semaphore_wait(barrier, T - 1 + B - 1)
+                for d in range(1, T):
+                    x_copy(s, d, 0, n // 2).start()
+                compute(s, n // 2, n)
+                for d in range(1, T):
+                    x_copy(s, d, n // 2, n - n // 2).start()
                 for d in range(1, B):
                     id_copy(d).start()
 
-            for d in range(1, T):
-                x_copy(s, d).start()
+            @pl.when(s > 0)
+            def _():
+                compute(s, 0, n)
+                for d in range(1, T):
+                    x_copy(s, d, 0, n).start()
 
         @pl.when(s == LX)
         def _():
@@ -287,7 +302,7 @@
     slots, size = occupied.shape[1:3]
     rows = size // T
     Q = chunks_of(2 * parts // B)
-    NB, LX, LY = min(6, Q), 3, 3
+    NB, LX, LY = min(6, Q), 2, 3
     n, blocks = parts // Q, freqs * rows // 8
     f32 = jnp.float32
     smem = pl.BlockSpec(memory_space=pltpu.SMEM)
@@ -299,9 +314,12 @@
     return pl.pallas_call(
         functools.partial(kernel, (pair_of(T, 2), pair_of(B, math.isqrt(B)), Q, NB, LX, LY)),
         out_shape=jax.ShapeDtypeStruct((freqs, CHI_DEV, rows, size), f32),
-        in_specs=[smem] * 3 + [vmem, hbm, hbm],
+        in_specs=[hbm, hbm, smem, hbm, hbm, hbm],
         out_specs=vmem,
         scratch_shapes=[
+            pltpu.SMEM((terms, parts), jnp.int32),
+            pltpu.SMEM((terms, parts), jnp.int32),
+            pltpu.VMEM((1, parts), jnp.int32),
             pltpu.VMEM((slots, size, size), occupied.dtype),
             pltpu.VMEM((slots, size, size), virtual.dtype),
             pltpu.VMEM((NB, T, n, rows, size), f32),
@@ -321,7 +339,7 @@
             dma((Q,)),
             dma((B,)),
             dma((B,)),
-            dma((3,)),
+            dma((6,)),
         ],
         compiler_params=pltpu.CompilerParams(
             collective_id=0, has_side_effects=True, vmem_limit_bytes=60 * 1024 * 1024

time: 167 us -> 162 us (0.970)
  Pallas kernels: 164 us -> 159 us
    pallas_call x1, Pallas kernels: 164 us -> 159 us  [body(): pl.pallas_call(functools.partial(kernel, (pair_of(T, 2), pair_of(B, math....]
where the time goes in v3:
time: 162 us; the launch traced here: 161 us
  Pallas kernels  159 us (98%)
  local copies, waits for them, and re-layouts  2.29 us (1%)
    pallas_call x1, Pallas kernels, body(): pl.pallas_call(functools.partial(kernel, (pair_of(T, 2), pair_of(B, math....  159 us

profile of v3, /device:TPU:1, one launch (start us, length us, event | category | flops | bytes accessed | tf_op | source)
XLA Modules:
  0.0 161.5 jit_solution(15028990093955410410)
XLA Ops:
  0.0 159.2 %products.1 = f32[4,32,16,128]{3,2,1,0:T(8,128)} custom-call(s32[16,192]{1,0:T(8,128)} %bitcast.7, s32[16,192]{1,0:T(8,128)} %bitcast.8, f32[4,8]{1,0:T(4,128)} %weights.1, s32[1,192]{1,0:T(1,128)} %bitcast.9, bf16[128,128,128]{2,1,0:T(8,128)(2,1)} %bitcast.5, bf16[128,128,128]{2,1,0:T(8,128)(2,1)} %bitcast.6), custom_call_target="tpu_custom_call" | custom-call | tf_op jit(solution)/shard_map/products/pallas_call | solution.py:314
  159.2 2.3 %copy.8 = f32[4,32,16,128]{3,2,1,0:T(8,128)} copy(f32[4,32,16,128]{3,2,1,0:T(8,128)} %products.1) | data formatting | bytes 2097152

commit v4 on v3

--- a/solution.py
+++ b/solution.py
@@ -10,6 +10,7 @@
 
 CHI_DEV = 32
 UNROLL = 2
+PAIR = 2
 MESH = pl.DeviceIdType.MESH
 
 
@@ -219,18 +220,22 @@
         lax.fori_loop(0, Q, one, 0)
 
     def reduce(q):
-        def one(c, carry):
-            want = c.astype(jnp.float32)
-            total = None
+        def some(step, carry):
+            cs = [step * PAIR + u for u in range(PAIR)]
+            wants = [c.astype(jnp.float32) for c in cs]
+            totals = [None] * PAIR
             for d in range(B):
-                same = jnp.broadcast_to(idwide[q, pl.ds(d, 1)], (8, cols)) == want
-                part = jnp.where(same[None], yrecv[q, d], 0.0)
-                total = part if total is None else total + part
-            total = total.reshape(freqs, rows, cols)
-            out[:, c] = jnp.where(q > 0, out[:, c], 0.0) + total
+                name = jnp.broadcast_to(idwide[q, pl.ds(d, 1)], (8, cols))
+                value = yrecv[q, d]
+                for u in range(PAIR):
+                    part = jnp.where((name == wants[u])[None], value, 0.0)
+                    totals[u] = part if totals[u] is None else totals[u] + part
+            for u in range(PAIR):
+                total = totals[u].reshape(freqs, rows, cols)
+                out[:, cs[u]] = jnp.where(q > 0, out[:, cs[u]], 0.0) + total
             return carry
 
-        lax.fori_loop(0, chi, one, 0)
+        lax.fori_loop(0, chi // PAIR, some, 0)
 
     def step(s, carry):
         @pl.when(s < Q)
@@ -307,7 +312,7 @@
     f32 = jnp.float32
     smem = pl.BlockSpec(memory_space=pltpu.SMEM)
     vmem = pl.BlockSpec(memory_space=pltpu.VMEM)
-    hbm = pl.BlockSpec(memory_space=pl.ANY)
+    hbm = pl.BlockSpec(memory_space=pltpu.HBM)
     dma = pltpu.SemaphoreType.DMA
     full = -(-parts // 128) * 128
     wide = max(full, Q * B)
@@ -342,14 +347,14 @@
             dma((6,)),
         ],
         compiler_params=pltpu.CompilerParams(
-            collective_id=0, has_side_effects=True, vmem_limit_bytes=60 * 1024 * 1024
+            collective_id=0, has_side_effects=True, vmem_limit_bytes=52 * 1024 * 1024
         ),
         name="products",
     )(
-        pair_occ.T,
-        pair_virt.T,
-        cos_weights,
-        partial_target_tile.reshape(1, parts),
+        pltpu.with_memory_space_constraint(pair_occ.T, pltpu.HBM),
+        pltpu.with_memory_space_constraint(pair_virt.T, pltpu.HBM),
+        pltpu.with_memory_space_constraint(cos_weights, pltpu.HBM),
+        pltpu.with_memory_space_constraint(partial_target_tile.reshape(1, parts), pltpu.HBM),
         occupied.reshape(slots, size, size),
         virtual.reshape(slots, size, size),
     )

time: 162 us -> 159 us (0.981)
  no operation moved by 1% of the time
where the time goes in v4:
time: 159 us
  Pallas kernels  158 us (99%)
    pallas_call x1, Pallas kernels, body(): pl.pallas_call(functools.partial(kernel, (pair_of(T, 2), pair_of(B, math....  158 us

profile of v4, /device:TPU:1, one launch (start us, length us, event | category | flops | bytes accessed | tf_op | source)
XLA Modules:
  0.0 159.1 jit_solution(5508794887858398555)
XLA Ops:
  0.0 158.1 %products.1 = f32[4,32,16,128]{3,2,1,0:T(8,128)S(1)} custom-call(s32[16,192]{1,0:T(8,128)} %bitcast.7, s32[16,192]{1,0:T(8,128)} %bitcast.8, f32[4,8]{1,0:T(4,128)} %weights.1, s32[1,192]{1,0:T(1,128)} %bitcast.9, bf16[128,128,128]{2,1,0:T(8,128)(2,1)} %bitcast.5, bf16[128,128,128]{2,1,0:T(8,128)(2,1)} %bitcast.6), custom_call_target="tpu_custom_call" | custom-call | tf_op jit(solution)/shard_map/products/pallas_call | solution.py:319
  158.1 1.0 copy.8

commit v5 on v4

--- a/solution.py
+++ b/solution.py
@@ -83,6 +83,7 @@
     t = lax.axis_index("tau")
     b = lax.axis_index("tile")
     near_t, near_b = offsets(tau), offsets(tile)
+    half = B // 2
 
     def tau_at(d):
         return around(t, near_t[d], tau)
@@ -157,7 +158,7 @@
             src_ref=ysend.at[buf, d - 1],
             dst_ref=yrecv.at[q, d],
             send_sem=ys.at[buf],
-            recv_sem=yr.at[q],
+            recv_sem=yr.at[q, int(d >= half)],
             device_id=(t, tile_at(d)),
             device_id_type=MESH,
         )
@@ -167,7 +168,17 @@
             src_ref=ysend.at[lax.rem(q, NB)],
             dst_ref=yrecv.at[q, pl.ds(1, B - 1)],
             send_sem=ys.at[lax.rem(q, NB)],
-            recv_sem=yr.at[q],
+            recv_sem=yr.at[q, 0],
+            device_id=(t, tile_at(1)),
+            device_id_type=MESH,
+        )
+
+    def y_part(q, lo, hi):
+        return pltpu.make_async_remote_copy(
+            src_ref=ysend.at[lax.rem(q, NB), pl.ds(lo - 1, hi - lo)],
+            dst_ref=yrecv.at[q, pl.ds(lo, hi - lo)],
+            send_sem=ys.at[lax.rem(q, NB)],
+            recv_sem=yr.at[q, int(lo >= half)],
             device_id=(t, tile_at(1)),
             device_id_type=MESH,
         )
@@ -219,12 +230,12 @@
 
         lax.fori_loop(0, Q, one, 0)
 
-    def reduce(q):
+    def reduce(q, lo, hi):
         def some(step, carry):
             cs = [step * PAIR + u for u in range(PAIR)]
             wants = [c.astype(jnp.float32) for c in cs]
             totals = [None] * PAIR
-            for d in range(B):
+            for d in range(lo, hi):
                 name = jnp.broadcast_to(idwide[q, pl.ds(d, 1)], (8, cols))
                 value = yrecv[q, d]
                 for u in range(PAIR):
@@ -232,7 +243,10 @@
                     totals[u] = part if totals[u] is None else totals[u] + part
             for u in range(PAIR):
                 total = totals[u].reshape(freqs, rows, cols)
-                out[:, cs[u]] = jnp.where(q > 0, out[:, cs[u]], 0.0) + total
+                kept = out[:, cs[u]]
+                if lo == 0:
+                    kept = jnp.where(q > 0, kept, 0.0)
+                out[:, cs[u]] = kept + total
             return carry
 
         lax.fori_loop(0, chi // PAIR, some, 0)
@@ -284,8 +298,10 @@
         @pl.when(s >= LX + LY)
         def _():
             q = s - LX - LY
-            y_all(q).wait_recv()
-            reduce(q)
+            y_part(q, 1, half).wait_recv()
+            reduce(q, 0, half)
+            y_part(q, half, B).wait_recv()
+            reduce(q, half, B)
 
         return carry
 
@@ -341,7 +357,7 @@
             dma((NB,)),
             dma((Q,)),
             dma((NB,)),
-            dma((Q,)),
+            dma((Q, 2)),
             dma((B,)),
             dma((B,)),
             dma((6,)),

time: 159 us -> 159 us (level)
  no operation moved by 1% of the time
where the time goes in v5:
time: 159 us
  Pallas kernels  158 us (99%)
    pallas_call x1, Pallas kernels, body(): pl.pallas_call(functools.partial(kernel, (pair_of(T, 2), pair_of(B, math....  158 us

profile of v5, /device:TPU:1, one launch (start us, length us, event | category | flops | bytes accessed | tf_op | source)
XLA Modules:
  0.0 158.5 jit_solution(5669755110629318436)
XLA Ops:
  0.0 157.5 %products.1 = f32[4,32,16,128]{3,2,1,0:T(8,128)S(1)} custom-call(s32[16,192]{1,0:T(8,128)} %bitcast.7, s32[16,192]{1,0:T(8,128)} %bitcast.8, f32[4,8]{1,0:T(4,128)} %weights.1, s32[1,192]{1,0:T(1,128)} %bitcast.9, bf16[128,128,128]{2,1,0:T(8,128)(2,1)} %bitcast.5, bf16[128,128,128]{2,1,0:T(8,128)(2,1)} %bitcast.6), custom_call_target="tpu_custom_call" | custom-call | tf_op jit(solution)/shard_map/products/pallas_call | solution.py:335
  157.5 1.0 copy.8
